TPU v7x, 256 devices: a 8x8x2 block of a 8x8x16 slice. The times are simulated.
256 devices in a mesh: groups: 2 (over z), seq: 128 (over x, y, core).
Axes of the slice: x: 8, y: 8, z: 2, core: 2. Of those that a mesh axis runs over, the one named last changes fastest.
The devices are a block of a 8x8x16 slice.
Arguments:
- latents: bfloat16 [2048, 64, 640], P(('groups', 'seq')), parts along dimension 0, may hold values from -6 to 6
- norm_gain: float32 [640], replicated, may hold values from 0.25 to 1.75
- norm_bias: float32 [640], replicated, may hold values from -3 to 3
- conv_weight: bfloat16 [5760, 640], P('seq'), may hold values from -0.078125 to 0.078125
- time_weight: bfloat16 [320, 640], replicated, may hold values from -0.3125 to 0.3125
- first_gain: float32 [640], replicated, may hold values from 0.25 to 1.75
- tconv_weight: bfloat16 [1920, 640], P('seq'), may hold values from -0.125 to 0.125
- second_gain: float32 [640], replicated, may hold values from 0.25 to 1.75
- qkv_weight: bfloat16 [640, 1920], P('seq'), may hold values from -0.25 to 0.25
- out_weight: bfloat16 [640, 640], P('seq'), may hold values from -0.25 to 0.25
- timesteps: int32 [8], P('groups'), parts along dimension 0, may hold values from 0 to 999
Outputs:
- mixed: bfloat16 [2048, 64, 640], P(('groups', 'seq')), parts along dimension 0
There are 2 independent parts, one for each index of `groups`. A program takes and returns all parts, laid end to end along the dimension named above; an argument that names none is the same for every part. Nothing has to cross between parts.
All inputs are finite; a program needn't handle non-finite values.
Results may differ from a plain program's by a relative error of at most 0.008.
Values may be sent and summed in bfloat16 or wider, within the bound.
A program may use at most 128 MiB of HBM per device.

v0:
```python
import functools

import jax
import jax.numpy as jnp
from jax import lax
from jax.sharding import Mesh
from jax.sharding import PartitionSpec as P

HEAD = 64
GROUPS = 32
TFEAT = 320
FRAMES = 16
SEQ = ("seq_0", "seq_1", "seq_2")
GROUPS_SEQ = ("groups", "seq_0", "seq_1", "seq_2")


def in_order(parts, dim):
    dims = list(parts.shape[1:])
    dims[dim] *= parts.shape[0]
    return jnp.moveaxis(parts, 0, dim).reshape(dims)


def one_gather(arrays, axis, dims):
    ravelled = jnp.concatenate([a.reshape(-1) for a in arrays])
    lines, at, gathered = (lax.all_gather(ravelled, axis), 0, [])
    for a, dim in zip(arrays, dims):
        parts = lines[:, at : at + a.size].reshape(-1, *a.shape)
        gathered.append(in_order(parts, dim))
        at += a.size
    return tuple(gathered)


def one_axis_at_a_time(shard, axes):
    return functools.reduce(lax.psum, axes, shard)


def from_behind(block, axis, distance):
    devices = range(lax.axis_size(axis))
    route = [(i - distance, i) for i in devices if i - distance in devices]
    return lax.ppermute(block, axis, route)


def time_embed(timesteps, time_weight):
    half = TFEAT // 2
    freqs = jnp.exp(-jnp.log(10000.0) * jnp.arange(half, dtype=jnp.float32) / half)
    angles = timesteps.astype(jnp.float32)[:, None] * freqs[None, :]
    feats = jnp.concatenate([jnp.cos(angles), jnp.sin(angles)], axis=-1)
    return jnp.dot(feats, time_weight.astype(jnp.float32))


def layer_norm(values):
    mean = jnp.mean(values, axis=-1, keepdims=True)
    centered = values - mean
    var = jnp.mean(centered * centered, axis=-1, keepdims=True)
    return centered * lax.rsqrt(var + 1e-05)


def temporal_block(spatial, first_gain, tconv_weight, second_gain, qkv_weight, out_weight):
    clips, frames, places, chans = spatial.shape
    heads = chans // HEAD
    values = spatial.astype(jnp.float32)
    first = (layer_norm(values) * first_gain).astype(jnp.bfloat16)
    zero = jnp.zeros_like(first[:, :1])
    before = jnp.concatenate([zero, first[:, :-1]], axis=1)
    after = jnp.concatenate([first[:, 1:], zero], axis=1)
    stacked = jnp.concatenate([before, first, after], axis=-1).reshape(-1, 3 * chans)
    mid = values + jnp.dot(stacked, tconv_weight, preferred_element_type=jnp.float32).reshape(
        values.shape
    )
    second = (layer_norm(mid) * second_gain).astype(jnp.bfloat16)
    qkv = jnp.dot(second.reshape(-1, chans), qkv_weight, preferred_element_type=jnp.float32).astype(
        jnp.bfloat16
    )
    qkv = qkv.reshape(clips, frames, places, 3, heads, HEAD)
    query, key, value = (qkv[:, :, :, 0], qkv[:, :, :, 1], qkv[:, :, :, 2])
    scores = jnp.einsum(
        "cfphd,cgphd->cphfg", query, key, preferred_element_type=jnp.float32
    ) * HEAD ** (-0.5)
    weights = jax.nn.softmax(scores, axis=-1).astype(jnp.bfloat16)
    attended = jnp.einsum(
        "cphfg,cgphd->cfphd", weights, value, preferred_element_type=jnp.float32
    ).astype(jnp.bfloat16)
    projected = jnp.dot(attended.reshape(-1, chans), out_weight, preferred_element_type=jnp.float32)
    return (mid + projected.reshape(mid.shape)).astype(jnp.bfloat16)


def shards(
    latents,
    norm_gain,
    norm_bias,
    conv_weight,
    time_weight,
    first_gain,
    tconv_weight,
    second_gain,
    qkv_weight,
    out_weight,
    timesteps,
):
    devices = lax.axis_size(SEQ)
    device = lax.axis_index(SEQ)
    clips = timesteps.shape[0]
    images = clips * FRAMES
    sharing = devices // images
    rows, width, chans = latents.shape
    height = sharing * rows
    image = device % images
    clip = image // FRAMES
    tconv_full, qkv_full, out_full = one_gather(
        (tconv_weight, qkv_weight, out_weight), SEQ, (0, 0, 0)
    )
    temb_all = time_embed(timesteps, time_weight)
    pick = (jnp.arange(clips) == clip).astype(jnp.float32)
    temb = jnp.sum(pick[:, None] * temb_all, axis=0)
    values = latents.astype(jnp.float32).reshape(rows * width, GROUPS, chans // GROUPS)
    partial_sums = jnp.stack([jnp.sum(values, axis=(0, 2)), jnp.sum(values * values, axis=(0, 2))])
    owner = (jnp.arange(images) == image).astype(jnp.float32)
    table = one_axis_at_a_time(owner[:, None, None] * partial_sums[None], SEQ)
    mine = jnp.sum(owner[:, None, None] * table, axis=0)
    entries = height * width * (chans // GROUPS)
    mean = mine[0] / entries
    var = mine[1] / entries - mean * mean
    normed = (values - mean[None, :, None]) * lax.rsqrt(var + 1e-05)[None, :, None]
    normed = normed.reshape(rows, width, chans) * norm_gain + norm_bias
    normed = jax.nn.silu(normed).astype(jnp.bfloat16)
    upper_rim = from_behind(normed[rows - 1 :], SEQ, images)
    lower_rim = from_behind(normed[:1], SEQ, -images)
    padded = jnp.concatenate([upper_rim, normed, lower_rim], axis=0)
    padded = jnp.pad(padded, ((0, 0), (1, 1), (0, 0)))
    taps = [padded[dy : dy + rows, dx : dx + width] for dy in range(3) for dx in range(3)]
    columns = jnp.concatenate(taps, axis=-1).reshape(rows * width, 9 * chans)
    base = latents.reshape(rows * width, chans).astype(jnp.float32) + temb[None, :]
    conv = jnp.dot(
        columns,
        lax.all_gather(conv_weight, SEQ, axis=0, tiled=True),
        preferred_element_type=jnp.float32,
    )
    spatial = (base + conv).astype(jnp.bfloat16)
    moved = lax.all_to_all(spatial, SEQ, split_axis=0, concat_axis=0, tiled=True)
    block = rows * width // devices
    places = sharing * block
    ordered = jnp.transpose(moved.reshape(sharing, clips, FRAMES, block, chans), (1, 2, 0, 3, 4))
    grouped = ordered.reshape(clips, FRAMES, places, chans)
    result = temporal_block(grouped, first_gain, tconv_full, second_gain, qkv_full, out_full)
    unordered = jnp.transpose(result.reshape(clips, FRAMES, sharing, block, chans), (2, 0, 1, 3, 4))
    returned = lax.all_to_all(
        unordered.reshape(rows * width, chans), SEQ, split_axis=0, concat_axis=0, tiled=True
    )
    return returned.reshape(rows, width, chans)


def solution(mesh):
    torus = Mesh(
        mesh.devices.reshape(mesh.shape["groups"], 8, 8, 2), ("groups", "seq_0", "seq_1", "seq_2")
    )
    return jax.shard_map(
        shards,
        mesh=torus,
        in_specs=(
            P(GROUPS_SEQ, None, None),
            P(),
            P(),
            P(SEQ, None),
            P(),
            P(),
            P(SEQ, None),
            P(),
            P(SEQ, None),
            P(SEQ, None),
            P("groups"),
        ),
        out_specs=P(GROUPS_SEQ, None, None),
        check_vma=False,
    )
```

profile of v0, /device:TPU:513, one launch (start us, length us, event | category | flops | bytes accessed | tf_op | source)
XLA Modules:
  0.0 346.2 jit_solution(1874407834715782001)
XLA Ops:
  12.4 24.3 %psum.21 = f32[64,2,32]{0,2,1:T(8,128)S(1)} all-reduce(f32[64,2,32]{0,2,1:T(8,128)S(1)} %broadcast_multiply_fusion.1), channel_id=1, replica_groups=mesh['groups'=2,'seq_0'=8,'seq_1'=8,'seq_2'=2] {'seq_0'}, use_global_device_ids=true, to_apply=%region_5.6 | all-reduce | flops 4096 | bytes 32768 | tf_op jit(solution)/shard_map/psum | solution.py:34
  36.7 33.6 %psum.22 = f32[64,2,32]{0,2,1:T(8,128)S(1)} all-reduce(f32[64,2,32]{0,2,1:T(8,128)S(1)} %psum.21), channel_id=1, replica_groups=mesh['groups'=2,'seq_0'=8,'seq_1'=8,'seq_2'=2] {'seq_1'}, use_global_device_ids=true, to_apply=%region_6.7 | all-reduce | flops 4096 | bytes 32768 | tf_op jit(solution)/shard_map/psum | solution.py:34
  70.3 20.2 %psum.23 = f32[64,2,32]{0,2,1:T(8,128)S(1)} all-reduce(f32[64,2,32]{0,2,1:T(8,128)S(1)} %psum.22), channel_id=1, replica_groups=mesh['groups'=2,'seq_0'=8,'seq_1'=8,'seq_2'=2] {'seq_2'}, use_global_device_ids=true, to_apply=%region_7.8 | all-reduce | flops 4096 | bytes 32768 | tf_op jit(solution)/shard_map/psum | solution.py:34
  92.2 2.6 collective-permute-start
  94.8 1.3 collective-permute-start.1
  96.6 1.9 collective-permute-done
  98.5 9.0 %collective-permute-done.1 = bf16[1,64,640]{2,1,0:T(8,128)(2,1)S(1)} collective-permute-done((bf16[1,64,640]{2,1,0:T(8,128)(2,1)S(1)}, bf16[1,64,640]{2,1,0:T(8,128)(2,1)S(1)}, u32[]{:S(2)}, u32[]{:S(2)}) %collective-permute-start.1) | collective-permute-done | bytes 81952 | tf_op jit(solution)/shard_map/ppermute | solution.py:40
  111.7 1.3 constant_dynamic-update-slice_fusion
  117.1 2.4 all-gather.8.cloned.1.call-done
  119.6 4.9 %copy.139 = bf16[128,1,22400]{2,0,1:T(8,128)(2,1)S(1)} copy(bf16[128,1,22400]{2,1,0:T(2,128)(2,1)} %all-gather.8.cloned.1.call-done) | data formatting | bytes 11468800
  124.4 2.4 copy-done.2
  126.9 76.5 %all-gather.6.cloned.1.call-done = bf16[128,45,640]{2,1,0:T(8,128)(2,1)} async-done(((bf16[1,45,640]{2,1,0:T(8,128)(2,1)}), bf16[128,45,640]{2,1,0:T(8,128)(2,1)}) %all-gather.6.cloned.1.call-update) | async-done | bytes 7372816 | tf_op jit(solution)/shard_map/all_gather | solution.py:135
  203.5 9.3 %reshape.157 = bf16[5760,640]{1,0:T(8,128)(2,1)} reshape(bf16[128,45,640]{2,1,0:T(8,128)(2,1)} %all-gather.6.cloned.1.call-done) | data formatting | bytes 14745600
  212.8 9.6 %fusion.24 = bf16[512,640]{1,0:T(8,128)(2,1)S(1)} fusion(f32[512,640]{1,0:T(8,128)S(1)} %bitcast_add_fusion, bf16[512,5760]{1,0:T(8,128)(2,1)} %bitcast.5, bf16[5760,640]{1,0:T(8,128)(2,1)} %reshape.157), kind=kOutput, calls=%fused_computation.28 | convolution fusion | flops 3775528960 | bytes 15237120 | tf_op jit(solution)/shard_map/dot_general | solution.py:133
  223.4 11.5 %all-to-all-start = ((bf16[128,4,640]{2,1,0:T(4,128)(2,1)}), bf16[128,4,640]{2,1,0:T(4,128)(2,1)}, u32[]{:S(2)}, u32[]{:S(2)}) async-start(bf16[128,4,640]{2,1,0:T(4,128)(2,1)} %all_to_all.12), calls=%async_computation | async-start | bytes 1310720 | tf_op jit(solution)/shard_map/all_to_all | solution.py:139
  234.9 4.2 %fusion.54 = (bf16[128,9600]{1,0:T(8,128)(2,1)S(1)}, bf16[128,9600]{1,0:T(8,128)(2,1)}) fusion(bf16[128,22400]{1,0:T(8,128)(2,1)} %bitcast.64), kind=kLoop, calls=%fused_computation.95 | loop fusion | bytes 9830400 | tf_op jit(solution)/shard_map/slice | solution.py:27
  239.1 6.1 %reshape.161 = bf16[1920,640,1,1]{1,0,2,3:T(8,128)(2,1)} reshape(bf16[128,9600]{1,0:T(8,128)(2,1)} %get-tuple-element.11) | data formatting | bytes 4915200 | tf_op jit(solution)/shard_map/reshape;reshape | solution.py:20
  245.1 3.5 %reshape_reshape.10 = bf16[640,1920]{1,0:T(8,128)(2,1)} reshape(bf16[128,9600]{1,0:T(8,128)(2,1)S(1)} %get-tuple-element.10) | data formatting | bytes 4915200 | tf_op jit(solution)/shard_map/reshape;reshape | solution.py:20
  249.2 7.5 %all-to-all-done = bf16[128,4,640]{2,1,0:T(4,128)(2,1)} async-done(((bf16[128,4,640]{2,1,0:T(4,128)(2,1)}), bf16[128,4,640]{2,1,0:T(4,128)(2,1)}, u32[]{:S(2)}, u32[]{:S(2)}) %all-to-all-start) | async-done | bytes 655392 | tf_op jit(solution)/shard_map/all_to_all | solution.py:139
  258.6 1.9 copy.98
  260.5 1.7 reshape.152
  264.4 3.2 fusion.58
  269.4 3.0 convolution_convert_fusion
  272.4 7.5 %reshape.148 = bf16[4,16,8,3,10,64]{5,4,3,2,1,0:T(8,128)(2,1)} reshape(bf16[512,1920]{1,0:T(8,128)(2,1)} %convolution_convert_fusion) | data formatting | bytes 3932160 | tf_op jit(solution)/shard_map/reshape | solution.py:74
  279.9 5.6 %fusion.53 = (bf16[4,16,8,1,10,64]{5,4,3,2,1,0:T(8,128)(2,1)S(1)}, bf16[4,16,8,1,10,64]{5,4,3,2,1,0:T(8,128)(2,1)S(1)}, bf16[4,16,8,1,10,64]{5,4,3,2,1,0:T(8,128)(2,1)S(1)}) fusion(bf16[4,16,8,3,10,64]{5,4,3,2,1,0:T(8,128)(2,1)} %reshape.148), kind=kLoop, calls=%fused_computation.94 | loop fusion | bytes 3932160 | tf_op jit(solution)/shard_map/slice | solution.py:75
  285.5 1.6 fusion.26
  287.1 11.1 %fusion.59 = (f32[4,8,10,16]{3,2,1,0:T(8,128)S(1)}, f32[4,8,10,16,16]{3,4,2,1,0:T(8,128)S(1)}) fusion(f32[4,8,10,16,16]{3,4,2,1,0:T(8,128)S(1)} %fusion.26), kind=kOutput, calls=%fused_computation.100 | output fusion | flops 327695 | bytes 675840 | tf_op jit(solution)/shard_map/sub | solution.py:79
  299.3 1.9 copy.110
  301.3 3.0 dot_general.29
  304.2 1.6 fusion.25
  305.8 1.6 reshape.149
  308.0 30.4 %all_to_all.18 = bf16[128,4,640]{2,1,0:T(4,128)(2,1)S(1)} all-to-all(bf16[128,4,640]{2,1,0:T(4,128)(2,1)S(1)} %copy.112), channel_id=1, replica_groups=mesh['groups'=2,'seq_0'=8,'seq_1'=8,'seq_2'=2] {'seq_0','seq_1','seq_2'}, dimensions={0} | all-to-all | bytes 1310720 | tf_op jit(solution)/shard_map/all_to_all | solution.py:146
  (85 shorter events, 26.0 us)
Async XLA Ops:
  6.5 89.8 %copy-start = (bf16[320,640]{1,0:T(8,128)(2,1)S(1)}, bf16[320,640]{1,0:T(8,128)(2,1)}, u32[]{:S(2)}) copy-start(bf16[320,640]{1,0:T(8,128)(2,1)} %param.15) | copy-start | bytes 1228804
  6.6 84.5 %copy-start.3 = (bf16[8,64,640]{2,1,0:T(8,128)(2,1)S(1)}, bf16[8,64,640]{2,1,0:T(8,128)(2,1)}, u32[]{:S(2)}) copy-start(bf16[8,64,640]{2,1,0:T(8,128)(2,1)} %param.11) | copy-start | bytes 1966084
  6.6 89.6 %copy-start.11 = (s32[4]{0:T(128)S(1)}, s32[4]{0:T(128)}, u32[]{:S(2)}) copy-start(s32[4]{0:T(128)} %param.21) | copy-start | bytes 52
  6.6 113.0 %all-gather.8.cloned.1.call-start = ((), (), s32[]{:S(2)}) async-start(), calls=%async_computation.3 | async-start | bytes 11558400 | tf_op jit(solution)/shard_map/all_gather | solution.py:25
  9.7 193.8 %all-gather.6.cloned.1.call-start = ((), (), s32[]{:S(2)}) async-start(), calls=%async_computation.2 | async-start | bytes 7925760 | tf_op jit(solution)/shard_map/all_gather | solution.py:135
  92.2 6.3 %collective-permute-start = (bf16[1,64,640]{2,1,0:T(8,128)(2,1)S(1)}, bf16[1,64,640]{2,1,0:T(8,128)(2,1)S(1)}, u32[]{:S(2)}, u32[]{:S(2)}) collective-permute-start(bf16[1,64,640]{2,1,0:T(8,128)(2,1)S(1)} %get-tuple-element.16), channel_id=1, source_target_pairs={{0,64},{1,65},{2,66},{3,67},{4,68},{5,69},{6,70},{7,71},{8,72},{9,... | collective-permute-start | bytes 245768 | tf_op jit(solution)/shard_map/ppermute | solution.py:40
  94.8 12.8 %collective-permute-start.1 = (bf16[1,64,640]{2,1,0:T(8,128)(2,1)S(1)}, bf16[1,64,640]{2,1,0:T(8,128)(2,1)S(1)}, u32[]{:S(2)}, u32[]{:S(2)}) collective-permute-start(bf16[1,64,640]{2,1,0:T(8,128)(2,1)S(1)} %get-tuple-element.17), channel_id=1, source_target_pairs={{64,0},{65,1},{66,2},{67,3},{68,4},{69,5},{70,6},{71,7},{72,8},{73... | collective-permute-start | bytes 245768 | tf_op jit(solution)/shard_map/ppermute | solution.py:40
  108.8 2.9 copy-start.7
  108.8 2.9 copy-start.8
  124.4 2.4 copy-start.2
  223.4 33.3 %all-to-all-start = ((bf16[128,4,640]{2,1,0:T(4,128)(2,1)}), bf16[128,4,640]{2,1,0:T(4,128)(2,1)}, u32[]{:S(2)}, u32[]{:S(2)}) async-start(bf16[128,4,640]{2,1,0:T(4,128)(2,1)} %all_to_all.12), calls=%async_computation | async-start | bytes 1310720 | tf_op jit(solution)/shard_map/all_to_all | solution.py:139
  260.5 1.8 copy-start.9
  262.3 1.1 copy-start.4
  262.3 2.1 copy-start.6
  264.4 3.6 %copy-start.10 = (f32[640]{0:T(1024)S(1)}, f32[640]{0:T(1024)}, u32[]{:S(2)}) copy-start(f32[640]{0:T(1024)} %param.18) | copy-start | bytes 7684
  267.7 1.7 copy-start.5
  307.5 31.9 %copy-start.1 = (bf16[320,640]{1,0:T(8,128)(2,1)S(1)}, bf16[320,640]{1,0:T(8,128)(2,1)}, u32[]{:S(2)}) copy-start(bf16[320,640]{1,0:T(8,128)(2,1)} %param.15) | copy-start | bytes 1228804
Sparse Core Ops, SparseCore 0:
  10.0 109.5 all-gather.7
  122.2 81.2 all-gather.5
where the time goes:
time: 348 us; the launch traced here: 346 us
  blocking collectives  109 us (31%)
  waiting for transfers between devices  98.1 us (28%)
  local copies, waits for them, and re-layouts  69.6 us (20%)
  matrix products  20.4 us (6%)
  other arithmetic  20.3 us (6%)
  starting transfers between devices  15.4 us (4%)
  between operations  13.9 us (4%)
    psum x3, blocking collectives, one_axis_at_a_time(): return functools.reduce(lax.psum, axes, shard)  78.2 us
    all_gather x1, waiting for transfers between devices, shards(): lax.all_gather(conv_weight, SEQ, axis=0, tiled=True)  76.5 us
    all_to_all x1, blocking collectives, shards(): lax.all_to_all(unordered.reshape(rows * width, chans), SEQ, split_axis=0,...  30.4 us
    unnamed x32, local copies, waits for them, and re-layouts  25.2 us
    all_to_all x1, starting transfers between devices, shards(): lax.all_to_all(spatial, SEQ, split_axis=0, concat_axis=0, tiled=True)  11.5 us
    sub x1, other arithmetic, temporal_block(): weights = jax.nn.softmax(scores, axis=-1).astype(jnp.bfloat16)  11.1 us
    ppermute x2, waiting for transfers between devices, from_behind(): return lax.ppermute(block, axis, route)  10.9 us
    another operation x3, local copies, waits for them, and re-layouts, in_order(): return jnp.moveaxis(parts, 0, dim).reshape(dims)  10.1 us
  transfers between devices with their start and end apart: 5, of which 5 were waited for; matrix products, arithmetic and copies ran while one was open for 9% of the time, Pallas kernels for 0%

commit v1 on v0

v1 whole, which is shorter than its diff:
```python
import functools

import jax
import jax.numpy as jnp
from jax import lax
from jax.experimental import pallas as pl
from jax.experimental.pallas import tpu as pltpu
from jax.sharding import Mesh
from jax.sharding import PartitionSpec as P

HEAD = 64
GROUPS = 32
TFEAT = 320
FRAMES = 16
C = 640
RING = 8
ROWS = 512
HALF = 256
WIDTH = 64
SEQ = ("seq_0", "seq_1", "seq_2")
GROUPS_SEQ = ("groups", "seq_0", "seq_1", "seq_2")
F32 = jnp.float32
BF16 = jnp.bfloat16
MESH = pl.DeviceIdType.MESH
HIGHEST = lax.Precision.HIGHEST

SLOTS = ((0, 0), (0, 1), (0, 2), (0, 3), (0, 4), (1, 1), (1, 2), (1, 3))
UPWARD_LAST = (0, 1, 2, 3)
STEPS = 9


def wrap(i):
    return lax.rem(i + 2 * RING, RING)


def iota(shape, dim):
    return lax.broadcasted_iota(jnp.int32, shape, dim)


def kernel(
    lat,
    gain,
    bias,
    convw,
    timew,
    gain1,
    tconvw,
    gain2,
    qkvw,
    outw,
    steps,
    out,
    slots,
    raw,
    wconv,
    wt,
    wqkv,
    wo,
    patches,
    halo_out,
    halo_in,
    stat_out,
    stat_in,
    spatial,
    grouped,
    stacked,
    mid,
    attended,
    mixed,
    line_send,
    line_recv,
    plane_send,
    plane_recv,
    twin_send,
    twin_recv,
    pair_send,
    pair_recv,
    go_send,
    go_recv,
    back_send,
    back_recv,
):
    x, y, c = (lax.axis_index(name) for name in SEQ)
    a = x + c * (y - x)
    b = y + c * (x - y)
    me = 2 * y + c
    across = {"seq_0": wrap(x + 4), "seq_1": y, "seq_2": c}
    twin = {"seq_0": x, "seq_1": y, "seq_2": 1 - c}

    def core_mate(a2, b2):
        return {"seq_0": a2 + c * (b2 - a2), "seq_1": b2 + c * (a2 - b2), "seq_2": c}

    def row_mate(j):
        return {"seq_0": x, "seq_1": lax.div(j, 2), "seq_2": lax.rem(j, 2)}

    barrier = pltpu.get_barrier_semaphore()
    greeted = [row_mate(lax.rem(me + d, FRAMES)) for d in range(1, FRAMES)]
    greeted += [{"seq_0": wrap(x + d), "seq_1": y, "seq_2": c} for d in (1, -1, 4)]
    for other in greeted:
        pl.semaphore_signal(barrier, inc=1, device_id=other, device_id_type=MESH)

    raw[...] = jnp.zeros_like(raw)
    raw[0:45] = convw[...]
    raw[48:63] = tconvw[...]
    for k in range(3):
        raw[64 + 16 * k : 69 + 16 * k] = qkvw[:, C * k : C * (k + 1)]
    raw[112:117] = outw[...]
    device = FRAMES * x + me
    to, frm = iota((96, 128), 0), iota((96, 128), 1)
    shifted = lax.rem(45 * device, 48) + frm
    shifted = jnp.where(shifted >= 48, shifted - 48, shifted)
    hit = (frm < 45) & (shifted == to) & (to < 48)
    hit |= (frm >= 48) & (frm < 63) & (to >= 48) & (to < 64) & (((15 * device + frm - 48) & 15) == to - 48)
    for k in range(4):
        start, low = 64 + 16 * k, 64 + 16 * (k // 2)
        there = (5 * device + frm - start + 8 * (k % 2)) & 15
        hit |= (frm >= start) & (frm < start + 5) & (to >= low) & (to < low + 16) & (there == to - low)
    placed = jnp.dot(hit.astype(F32).astype(BF16), raw[...], preferred_element_type=F32).astype(BF16)
    slots[0, c, a, b] = placed[:48]
    slots[1, c, a, b] = placed[48:]

    sums, squares = jnp.zeros((1, C), F32), jnp.zeros((1, C), F32)
    for r in range(8):
        v = lat[WIDTH * r : WIDTH * (r + 1)].astype(F32)
        sums += jnp.sum(v, axis=0, keepdims=True)
        squares += jnp.sum(v * v, axis=0, keepdims=True)
    stat_row = iota((8, C), 0)
    stat_out[...] = jnp.where(stat_row == 0, sums, 0.0) + jnp.where(stat_row == 1, squares, 0.0)

    pl.semaphore_wait(barrier, len(greeted))

    sent = []

    def send(src, dst, send_sem, recv_sem, other):
        copy = pltpu.make_async_remote_copy(
            src_ref=src, dst_ref=dst, send_sem=send_sem, recv_sem=recv_sem, device_id=other, device_id_type=MESH
        )
        copy.start()
        sent.append(copy)

    def arrived(ref, sem):
        pltpu.make_async_copy(ref, ref, sem).wait()

    def slot_b(i):
        way, hops = SLOTS[i]
        return wrap(b + (hops if way else -hops))

    def along_line(part, i, way):
        hops = SLOTS[i][1] + 1
        ref = slots.at[part, c, a, slot_b(i)]
        n = (hops - 1) if way == 0 else (3 + hops)
        send(ref, ref, line_send.at[part, n], line_recv.at[part, n], core_mate(a, wrap(b + (-1 if way else 1))))

    def line_arrived(part, i):
        way, hops = SLOTS[i]
        n = (hops - 1) if way == 0 else (3 + hops)
        ref = slots.at[part, c, a, slot_b(i)]
        arrived(ref, line_recv.at[part, n])

    def block_a(way, k):
        return wrap(a + (k if way else -k))

    def along_plane(part, i, way, k):
        ref = slots.at[part, c, block_a(way, k - 1), slot_b(i)]
        sems = (plane_send.at[part, way, k - 1, i], plane_recv.at[part, way, k - 1, i])
        send(ref, ref, *sems, core_mate(wrap(a + (-1 if way else 1)), b))

    def plane_arrived(part, i, way, k):
        ref = slots.at[part, c, block_a(way, k), slot_b(i)]
        arrived(ref, plane_recv.at[part, way, k - 1, i])

    def to_twin(part, n, block):
        ref = slots.at[part, c, block]
        send(ref, ref, twin_send.at[part, n], twin_recv.at[part, n], twin)

    def ring_step(part, t):
        for i, (way, hops) in enumerate(SLOTS):
            k = t - hops + 1
            if k == 1:
                if i == 0:
                    along_line(part, 0, 0)
                    along_line(part, 0, 1)
                else:
                    line_arrived(part, i)
                    if hops < (3 if way else 4):
                        along_line(part, i, way)
                along_plane(part, i, 0, 1)
                along_plane(part, i, 1, 1)
            elif 2 <= k <= 4:
                for w in (0, 1):
                    plane_arrived(part, i, w, k - 1)
                    if k < 4 or (i in UPWARD_LAST) == (w == 0):
                        along_plane(part, i, w, k)
            elif k == 5:
                plane_arrived(part, i, 0 if i in UPWARD_LAST else 1, 4)
        if t == 4:
            to_twin(part, 0, a)
        elif t in (5, 6, 7):
            to_twin(part, 2 * (t - 4) - 1, block_a(0, t - 4))
            to_twin(part, 2 * (t - 4), block_a(1, t - 4))
        elif t == 8:
            to_twin(part, 7, block_a(0, 4))

    def twin_arrived(part):
        for n, far in enumerate((0, -1, 1, -2, 2, -3, 3, 4)):
            ref = slots.at[part, 1 - c, wrap(b + far)]
            arrived(ref, twin_recv.at[part, n])

    def step(s):
        if s < STEPS:
            ring_step(0, s)
        if 0 <= s - 5 < STEPS:
            ring_step(1, s - 5)

    step(0)
    send(stat_out, stat_in, pair_send.at[0], pair_recv.at[0], across)
    step(1)

    arrived(stat_in, pair_recv.at[0])
    member = (iota((C, 128), 0) >= 20 * iota((C, 128), 1)) & (iota((C, 128), 0) < 20 * iota((C, 128), 1) + 20)
    back = (iota((128, C), 1) >= 20 * iota((128, C), 0)) & (iota((128, C), 1) < 20 * iota((128, C), 0) + 20)
    totals = stat_out[...] + stat_in[...]
    entries = 2 * ROWS * (C // GROUPS)
    by_group = jnp.dot(totals, member.astype(F32), precision=HIGHEST, preferred_element_type=F32) / entries
    mean_g = by_group[0:1]
    rstd_g = lax.rsqrt(by_group[1:2] - mean_g * mean_g + 1e-05)
    row8 = iota((8, 128), 0)
    both = jnp.where(row8 == 0, mean_g, 0.0) + jnp.where(row8 == 1, rstd_g, 0.0)
    spread = jnp.dot(both, back.astype(F32), precision=HIGHEST, preferred_element_type=F32)
    scale = spread[1:2] * gain[...]
    offset = bias[...] - spread[0:1] * scale
    column = iota((WIDTH, C), 0)

    def with_shifts(v, at):
        patches[pl.ds(at, WIDTH), C : 2 * C] = v.astype(BF16)
        patches[pl.ds(at, WIDTH), 0:C] = jnp.where(column == 0, 0.0, pltpu.roll(v, 1, 0)).astype(BF16)
        after = jnp.where(column == WIDTH - 1, 0.0, pltpu.roll(v, WIDTH - 1, 0))
        patches[pl.ds(at, WIDTH), 2 * C : 3 * C] = after.astype(BF16)

    def norm_row(r, carry):
        at = pl.multiple_of(WIDTH * r, WIDTH)
        v = lat[pl.ds(at, WIDTH)].astype(F32) * scale + offset
        v = v / (1.0 + jnp.exp(-v))
        with_shifts(v, pl.multiple_of(at + WIDTH, WIDTH))
        return carry

    lax.fori_loop(0, 8, norm_row, 0)
    lower = lax.div(x, 4)
    edge = pl.multiple_of(ROWS - (ROWS - WIDTH) * lower, WIDTH)
    halo_out[...] = patches[pl.ds(edge, WIDTH), C : 2 * C]
    send(halo_out, halo_in, pair_send.at[1], pair_recv.at[1], across)
    step(2)

    clip = lax.rem(x, 4)
    t = steps[clip].astype(F32)
    freqs = jnp.exp(iota((8, TFEAT // 2), 1).astype(F32) * (-jnp.log(F32(10000.0)) / (TFEAT // 2)))
    angles = t * freqs
    half = TFEAT // 2
    temb = jnp.dot(jnp.cos(angles), timew[:half].astype(F32), precision=HIGHEST, preferred_element_type=F32)
    temb += jnp.dot(jnp.sin(angles), timew[half:].astype(F32), precision=HIGHEST, preferred_element_type=F32)
    temb = temb[0:1]

    arrived(halo_in, pair_recv.at[1])
    inner = pl.multiple_of((ROWS + WIDTH) * (1 - lower), WIDTH)
    outer = pl.multiple_of((ROWS + WIDTH) * lower, WIDTH)
    with_shifts(halo_in[...].astype(F32), inner)
    patches[pl.ds(outer, WIDTH), :] = jnp.zeros((WIDTH, 3 * C), BF16)

    for s in range(3, STEPS):
        step(s)
    twin_arrived(0)

    lane_row = iota((16, C), 0)

    def slot(part, j, xb, tile):
        y2 = j // 2
        at = (part, 0, xb, y2) if j % 2 == 0 else (part, 1, y2, xb)
        return slots[at + (slice(16 * tile, 16 * tile + 16),)]

    def tile_rows(part, each, row0, xb, tile, flip):
        rows = (lane_row ^ 8) if flip else lane_row
        first = row0 // each
        value = slot(part, first, xb, tile).astype(F32)
        for j in range(first + 1, (row0 + 15) // each + 1):
            value = jnp.where(rows >= each * j - row0, slot(part, j, xb, tile).astype(F32), value)
        if flip:
            value = jnp.concatenate([value[8:], value[:8]], axis=0)
        return value.astype(BF16)

    def conv_block(xb, carry):
        for n in range(45):
            at = pl.multiple_of(720 * xb + 16 * n, 16)
            wconv[pl.ds(at, 16)] = tile_rows(0, 45, 16 * n, xb, n % 3, False)
        return carry

    lax.fori_loop(0, RING, conv_block, 0)

    def conv_half(g, between):
        total = lat[HALF * g : HALF * (g + 1)].astype(F32) + temb
        for dy in range(3):
            total += jnp.dot(
                patches[HALF * g + WIDTH * dy : HALF * (g + 1) + WIDTH * dy],
                wconv[3 * C * dy : 3 * C * (dy + 1)],
                preferred_element_type=F32,
            )
            between(dy)
        spatial[HALF * g : HALF * (g + 1)] = total.astype(BF16)

    order = (8, 7, 9, 6, 10, 5, 11, 4, 12, 3, 13, 2, 14, 1, 15)

    def exchange(g):
        mine = pl.multiple_of(16 * me, 16)
        for d in order:
            j = lax.rem(me + d, FRAMES)
            src = spatial.at[pl.ds(pl.multiple_of(HALF * g + 16 * j, 16), 16)]
            send(src, grouped.at[g, pl.ds(mine, 16)], go_send.at[g, d], go_recv.at[g, d], row_mate(j))
        grouped[g, pl.ds(mine, 16)] = spatial[pl.ds(pl.multiple_of(HALF * g + mine, 16), 16)]

    conv_half(0, lambda dy: step(9 + dy) if dy < 2 else None)
    exchange(0)
    conv_half(1, lambda dy: step(11 + dy) if dy < 2 else None)
    exchange(1)
    step(13)
    twin_arrived(1)

    def rest_block(xb, carry):
        for n in range(15):
            at = pl.multiple_of(240 * xb + 16 * n, 16)
            wt[pl.ds(at, 16)] = tile_rows(1, 15, 16 * n, xb, 0, False)
        for n in range(5):
            at = pl.multiple_of(80 * xb + 16 * n, 16)
            wqkv[pl.ds(at, 16), 0:C] = tile_rows(1, 5, 16 * n, xb, 1, False)
            wqkv[pl.ds(at, 16), C : 2 * C] = tile_rows(1, 5, 16 * n, xb, 1, True)
            wqkv[pl.ds(at, 16), 2 * C :] = tile_rows(1, 5, 16 * n, xb, 2, False)
            wo[pl.ds(at, 16)] = tile_rows(1, 5, 16 * n, xb, 2, True)
        return carry

    lax.fori_loop(0, RING, rest_block, 0)

    def layer_norm(v):
        centered = v - jnp.sum(v, axis=-1, keepdims=True) * (1.0 / C)
        var = jnp.sum(centered * centered, axis=-1, keepdims=True) * (1.0 / C)
        return centered * lax.rsqrt(var + 1e-05)

    apart = (iota((16, HALF), 0) - iota((16, HALF), 1)) & 15
    mask = jnp.where(apart == 0, 0.0, -1e30).astype(F32)
    low_head = iota((HALF, 2 * HEAD), 1) < HEAD

    def temporal(g):
        values = grouped[g].astype(F32)
        first = (layer_norm(values) * gain1[...]).astype(BF16)
        stacked[0:16, 0:C] = jnp.zeros((16, C), BF16)
        stacked[16:HALF, 0:C] = first[: HALF - 16]
        stacked[:, C : 2 * C] = first
        stacked[0 : HALF - 16, 2 * C :] = first[16:]
        stacked[HALF - 16 :, 2 * C :] = jnp.zeros((16, C), BF16)
        mid[...] = values + jnp.dot(stacked[...], wt[...], preferred_element_type=F32)
        second = (layer_norm(mid[...]) * gain2[...]).astype(BF16)
        stacked[...] = jnp.dot(second, wqkv[...], preferred_element_type=F32).astype(BF16)
        for h in range(C // (2 * HEAD)):
            at = 2 * HEAD * h
            query = stacked[:, at : at + 2 * HEAD]
            key = stacked[:, C + at : C + at + 2 * HEAD]
            value = stacked[:, 2 * C + at : 2 * C + at + 2 * HEAD]
            wide = query.astype(F32)
            heads = [jnp.where(low_head, wide, 0.0), jnp.where(low_head, 0.0, wide)]
            both = jnp.concatenate(heads, axis=0).astype(BF16)
            scores = lax.dot_general(both, key, (((1,), (1,)), ((), ())), preferred_element_type=F32)
            scores = scores.reshape(2 * FRAMES, 16, HALF) * HEAD ** (-0.5) + mask[None]
            scores = scores.reshape(2 * HALF, HALF)
            top = jnp.max(scores, axis=-1, keepdims=True)
            expd = jnp.exp(scores - top)
            weights = (expd / jnp.sum(expd, axis=-1, keepdims=True)).astype(BF16)
            got = jnp.dot(weights, value, preferred_element_type=F32)
            attended[:, at : at + 2 * HEAD] = jnp.where(low_head, got[:HALF], got[HALF:]).astype(BF16)
        projected = jnp.dot(attended[...], wo[...], preferred_element_type=F32)
        mixed[g] = (mid[...] + projected).astype(BF16)

    def give_back(g):
        mine = pl.multiple_of(HALF * g + 16 * me, 16)
        for d in order:
            j = lax.rem(me + d, FRAMES)
            src = mixed.at[g, pl.ds(pl.multiple_of(16 * j, 16), 16)]
            send(src, out.at[pl.ds(mine, 16)], back_send.at[g, d], back_recv.at[g, d], row_mate(j))
        out[pl.ds(mine, 16)] = mixed[g, pl.ds(pl.multiple_of(16 * me, 16), 16)]

    for g in (0, 1):
        for d in order:
            j = lax.rem(me - d + FRAMES, FRAMES)
            arrived(grouped.at[g, pl.ds(pl.multiple_of(16 * j, 16), 16)], go_recv.at[g, d])
        temporal(g)
        give_back(g)
    for g in (0, 1):
        for d in order:
            j = lax.rem(me - d + FRAMES, FRAMES)
            arrived(out.at[pl.ds(pl.multiple_of(HALF * g + 16 * j, 16), 16)], back_recv.at[g, d])
    for copy in sent:
        copy.wait_send()


def shards(
    latents,
    norm_gain,
    norm_bias,
    conv_weight,
    time_weight,
    first_gain,
    tconv_weight,
    second_gain,
    qkv_weight,
    out_weight,
    timesteps,
):
    rows, width, chans = latents.shape
    vmem = pl.BlockSpec(memory_space=pltpu.VMEM)
    dma = pltpu.SemaphoreType.DMA
    result = pl.pallas_call(
        kernel,
        out_shape=jax.ShapeDtypeStruct((rows * width, chans), BF16),
        in_specs=[vmem] * 10 + [pl.BlockSpec(memory_space=pltpu.SMEM)],
        out_specs=vmem,
        scratch_shapes=[
            pltpu.VMEM((2, 2, RING, RING, 48, C), BF16),
            pltpu.VMEM((128, C), BF16),
            pltpu.VMEM((9 * C, C), BF16),
            pltpu.VMEM((3 * C, C), BF16),
            pltpu.VMEM((C, 3 * C), BF16),
            pltpu.VMEM((C, C), BF16),
            pltpu.VMEM((ROWS + 2 * WIDTH, 3 * C), BF16),
            pltpu.VMEM((WIDTH, C), BF16),
            pltpu.VMEM((WIDTH, C), BF16),
            pltpu.VMEM((8, C), F32),
            pltpu.VMEM((8, C), F32),
            pltpu.VMEM((ROWS, C), BF16),
            pltpu.VMEM((2, HALF, C), BF16),
            pltpu.VMEM((HALF, 3 * C), BF16),
            pltpu.VMEM((HALF, C), F32),
            pltpu.VMEM((HALF, C), BF16),
            pltpu.VMEM((2, HALF, C), BF16),
            dma((2, 7)),
            dma((2, 7)),
            dma((2, 2, 4, 8)),
            dma((2, 2, 4, 8)),
            dma((2, 8)),
            dma((2, 8)),
            dma((2,)),
            dma((2,)),
            dma((2, FRAMES)),
            dma((2, FRAMES)),
            dma((2, FRAMES)),
            dma((2, FRAMES)),
        ],
        compiler_params=pltpu.CompilerParams(
            collective_id=0, has_side_effects=True, vmem_limit_bytes=63 * 2**20
        ),
    )(
        latents.reshape(rows * width, chans),
        norm_gain.reshape(1, chans),
        norm_bias.reshape(1, chans),
        conv_weight,
        time_weight,
        first_gain.reshape(1, chans),
        tconv_weight,
        second_gain.reshape(1, chans),
        qkv_weight,
        out_weight,
        timesteps,
    )
    return result.reshape(rows, width, chans)


def solution(mesh):
    torus = Mesh(
        mesh.devices.reshape(mesh.shape["groups"], 8, 8, 2), ("groups", "seq_0", "seq_1", "seq_2")
    )
    return jax.shard_map(
        shards,
        mesh=torus,
        in_specs=(
            P(GROUPS_SEQ, None, None),
            P(),
            P(),
            P(SEQ, None),
            P(),
            P(),
            P(SEQ, None),
            P(),
            P(SEQ, None),
            P(SEQ, None),
            P("groups"),
        ),
        out_specs=P(GROUPS_SEQ, None, None),
        check_vma=False,
    )
```

time: 348 us -> 119 us (0.34)
  Pallas kernels: 0 us -> 114 us
  blocking collectives: 109 us -> 0 us
  waiting for transfers between devices: 98.1 us -> 0 us
  local copies, waits for them, and re-layouts: 69.6 us -> 5.22 us
  matrix products: 20.4 us -> 0 us
  other arithmetic: 20.3 us -> 0 us
  starting transfers between devices: 15.4 us -> 0 us
  between operations: 13.9 us -> 0.01 us
    pallas_call x0 -> x1, Pallas kernels: none -> 114 us  [shards(): pl.pallas_call(kernel, out_shape=jax.ShapeDtypeStruct((rows * width, chan...]
    all_gather x2 -> x0, waiting for transfers between devices: 79 us -> none  [the longest x1 76.5 us: shards(): lax.all_gather(conv_weight, SEQ, axis=0, tiled=True)]
    psum x3 -> x0, blocking collectives: 78.2 us -> none  [one_axis_at_a_time(): return functools.reduce(lax.psum, axes, shard)]
    all_to_all x1 -> x0, blocking collectives: 30.4 us -> none  [shards(): lax.all_to_all(unordered.reshape(rows * width, chans), SEQ, split_axis=0,...]
    unnamed x32 -> x7, local copies, waits for them, and re-layouts: 25.2 us -> 2.19 us
    dot_general x7 -> x0, matrix products: 20.4 us -> none  [the longest x1 9.61 us: shards(): jnp.dot(columns, lax.all_gather(conv_weight, SEQ, axis=0, tiled=True), pr...]
    all_to_all x1 -> x0, starting transfers between devices: 11.5 us -> none  [shards(): lax.all_to_all(spatial, SEQ, split_axis=0, concat_axis=0, tiled=True)]
    sub x1 -> x0, other arithmetic: 11.1 us -> none  [temporal_block(): weights = jax.nn.softmax(scores, axis=-1).astype(jnp.bfloat16)]
  transfers between devices with their start and end apart: 5 -> 0, of which waited for: 5 -> 0; matrix products, arithmetic and copies ran while one was open for 9% -> 0% of each run, Pallas kernels for 0% -> 0%
where the time goes in v1:
time: 119 us
  Pallas kernels  114 us (96%)
  local copies, waits for them, and re-layouts  5.22 us (4%)
    pallas_call x1, Pallas kernels, shards(): pl.pallas_call(kernel, out_shape=jax.ShapeDtypeStruct((rows * width, chan...  114 us

profile of v1, /device:TPU:513, one launch (start us, length us, event | category | flops | bytes accessed | tf_op | source)
XLA Modules:
  0.0 118.9 jit_solution(12105840584252060707)
XLA Ops:
  0.0 0.0 copy-start
  0.0 1.3 %reshape.19.gain = f32[1,640]{1,0:T(1,128)} reshape(f32[640]{0:T(1024)} %param.12) | data formatting | bytes 5120 | tf_op jit(solution)/shard_map/reshape | solution.py:458
  1.3 0.0 copy-done
  1.3 0.0 copy-start.1
  1.3 0.6 reshape.20.bias
  1.9 0.1 copy-done.1
  2.0 0.0 copy-start.2
  2.0 0.6 reshape.21.gain1
  2.6 0.1 copy-done.2
  2.7 0.6 reshape.22.gain2
  3.2 113.6 %shard_map.109 = bf16[512,640]{1,0:T(8,128)(2,1)} custom-call(bf16[512,640]{1,0:T(8,128)(2,1)} %bitcast.3, f32[1,640]{1,0:T(1,128)} %reshape.19.gain, f32[1,640]{1,0:T(1,128)} %reshape.20.bias, bf16[45,640]{1,0:T(8,128)(2,1)} %convw.1, bf16[320,640]{1,0:T(8,128)(2,1)} %timew.1, f32[1,640]{1,0:T(1,128)} %reshape.21.gain1, bf16[15,640]{1,0:T(8,128)(2,1)} %tconvw.1, ...), custom_call_target="tpu_custom_call" | custom-call | tf_op jit(solution)/shard_map/pallas_call | solution.py:417
  116.9 2.0 %copy.13 = bf16[8,64,640]{2,1,0:T(8,128)(2,1)} copy(bf16[8,64,640]{2,1,0:T(8,128)(2,1)} %bitcast.2) | data formatting | bytes 1310720
Async XLA Ops:
  0.0 1.3 %copy-start = (f32[640]{0:T(1024)S(1)}, f32[640]{0:T(1024)}, u32[]{:S(2)}) copy-start(f32[640]{0:T(1024)} %param.13) | copy-start | bytes 7684
  1.3 0.7 copy-start.1
  2.0 0.7 copy-start.2
